TPU v7x, 32 devices: a whole 2x2x4 slice. The times are simulated.
32 devices in a mesh: rep: 4 (over x, core), mx: 2 (over y), my: 4 (over z).
Axes of the slice: x: 2, y: 2, z: 4, core: 2. Of those that a mesh axis runs over, the one named last changes fastest.
Arguments:
- coefficients: bfloat16 [2, 384, 384, 384], P(None, 'mx', 'my'), may hold values from -7.5 to 7.5
- noise_field: bfloat16 [128, 2, 1536, 1536], P(('rep', 'mx'), None, 'my'), may hold values from -96 to 96
- mode_table: bfloat16 [384, 1536], replicated, may hold values from -0.3125 to 0.3125
Outputs:
- update: bfloat16 [2, 384, 384, 384], P(None, 'mx', 'my', 'rep')
All inputs are finite; a program needn't handle non-finite values.
Results may differ from a plain program's by a relative error of at most 0.008.
Values may be sent and summed in bfloat16 or wider, within the bound.
A program may use at most 384 MiB of HBM per device.

v0:
```python
import jax
import jax.numpy as jnp
from jax import lax
from jax.sharding import PartitionSpec as P

DAMPING = 0.25


def body(coefficients, noise_field, mode_table):
    rep_index = lax.axis_index("rep")
    col_index = lax.axis_index("my")
    rep_count = lax.axis_size("rep")
    row_count = lax.axis_size("mx")
    col_count = lax.axis_size("my")
    planes_dev = noise_field.shape[0]
    planes_rep = planes_dev * row_count
    planes_all = planes_rep * rep_count
    mode_count = mode_table.shape[0]
    point_count = mode_table.shape[1]
    slab_first = point_count // 2 - planes_all // 2
    row_block = mode_count // row_count
    col_block = mode_count // col_count
    point_block = point_count // col_count
    own_block = mode_count // rep_count
    slab_own = lax.dynamic_slice_in_dim(
        mode_table, slab_first + rep_index * planes_rep, planes_rep, 1
    )
    zmodes = jnp.einsum(
        "pabk,kz->zpba", coefficients, slab_own, preferred_element_type=jnp.float32
    ).astype(jnp.bfloat16)
    zmodes = zmodes.reshape(planes_rep, 2, col_block * row_block)
    spread = lax.all_to_all(zmodes, "mx", split_axis=0, concat_axis=2, tiled=True)
    grouped = spread.reshape(planes_dev, 2, row_count, col_block, row_block)
    tiled_table = mode_table.reshape(row_count, row_block, point_count)
    own_points = lax.dynamic_slice_in_dim(tiled_table, col_index * point_block, point_block, 2)
    block_part = jnp.einsum(
        "zpsal,slx->zpax",
        lax.all_gather(grouped, "my", axis=3, tiled=True),
        own_points,
        preferred_element_type=jnp.float32,
    ).astype(jnp.bfloat16)
    wave_field = jnp.einsum(
        "zpax,ay->zpxy", block_part, mode_table, preferred_element_type=jnp.float32
    )
    wave_real = wave_field[:, 0]
    wave_imag = wave_field[:, 1]
    density = wave_real * wave_real + wave_imag * wave_imag
    noise_wide = noise_field.astype(jnp.float32)
    drive_term = jnp.stack(
        [
            density * (wave_imag - DAMPING * wave_real) + noise_wide[:, 0],
            density * (-wave_real - DAMPING * wave_imag) + noise_wide[:, 1],
        ],
        1,
    ).astype(jnp.bfloat16)
    proj_columns = jnp.einsum(
        "zpxy,ny->zpnx", drive_term, mode_table, preferred_element_type=jnp.float32
    ).astype(jnp.bfloat16)
    block_part = lax.all_to_all(proj_columns, "my", split_axis=2, concat_axis=3, tiled=True)
    folded = jnp.einsum(
        "zpax,slx->zpsal", block_part, tiled_table, preferred_element_type=jnp.float32
    ).astype(jnp.bfloat16)
    proj_rows = folded.reshape(
        block_part.shape[0], block_part.shape[1], row_count * col_block * row_block
    )
    gathered_rows = lax.all_to_all(proj_rows, "mx", split_axis=2, concat_axis=0, tiled=True)
    slab_back = lax.dynamic_slice_in_dim(mode_table, rep_index * own_block, own_block, 0)[
        :, slab_first : slab_first + planes_all
    ]
    portion = lax.all_gather(gathered_rows, "rep", axis=0, tiled=True)
    plane_grid = portion.reshape(portion.shape[0], 2, col_block, row_block)
    summed = jnp.einsum("zpba,nz->pabn", plane_grid, slab_back, preferred_element_type=jnp.float32)
    return summed.astype(jnp.bfloat16)


def solution(mesh):
    in_specs = (P(None, "mx", "my", None), P(("rep", "mx"), None, "my", None), P())
    out_specs = P(None, "mx", "my", "rep")
    return jax.shard_map(body, mesh=mesh, in_specs=in_specs, out_specs=out_specs, check_vma=False)
```

profile of v0, /device:TPU:0, one launch (start us, length us, event | category | flops | bytes accessed | tf_op | source)
XLA Modules:
  0.0 974.2 jit_solution(4171945368356783076)
XLA Ops:
  6.5 0.0 copy-start
  6.5 0.0 all-gather.3.cloned.1.call-start
  6.5 1.3 copy-done
  7.8 25.5 %convert_bitcast_fusion.3 = bf16[32,2,96,192]{2,0,3,1:T(8,128)(2,1)} fusion(bf16[2,192,96,384]{3,2,1,0:T(8,128)(2,1)} %param.3, bf16[384,1536]{1,0:T(8,128)(2,1)S(1)} %copy-done, s32[]{:T(128)S(6)} %select_n.10), kind=kOutput, calls=%fused_computation.17 | convolution fusion | flops 907149312 | bytes 30769156 | tf_op jit(solution)/shard_map/pabk,kz->zpba/dot_general | solution.py:28
  33.3 5.1 copy.45
  38.5 6.9 reshape.28
  45.3 31.8 %all_to_all.51 = bf16[32,2,18432]{2,1,0:T(2,128)(2,1)S(1)} all-to-all(bf16[32,2,18432]{2,1,0:T(2,128)(2,1)S(1)} %reshape.28), channel_id=1, replica_groups=mesh['rep'=4,'mx'=2,'my'=4] {'mx'}, dimensions={0} | all-to-all | bytes 4718592 | tf_op jit(solution)/shard_map/all_to_all | solution.py:32
  77.1 2.4 copy.52
  79.5 4.5 reshape.17
  84.0 0.0 all-gather.3.cloned.1.call-update
  84.0 0.2 all-gather.5.cloned.1.call-start
  84.2 37.8 %convert_element_type.34 = f32[16,2,384,1536]{3,2,1,0:T(8,128)} convert(bf16[16,2,384,1536]{3,2,1,0:T(8,128)(2,1)} %param.4) | non-fusion elementwise | flops 18874368 | bytes 113246208 | tf_op jit(solution)/shard_map/convert_element_type | solution.py:48
  122.1 180.8 %all-gather.3.cloned.1.call-done = bf16[16,2,2,384,192]{4,3,2,1,0:T(8,128)(2,1)} async-done(((bf16[16,2,2,96,192]{4,3,2,1,0:T(8,128)(2,1)}), bf16[16,2,2,384,192]{4,3,2,1,0:T(8,128)(2,1)}) %all-gather.3.cloned.1.call-update) | async-done | bytes 9437200 | tf_op jit(solution)/shard_map/all_gather | solution.py:38
  302.9 36.1 %fusion.6 = f32[16,2,384,1536]{3,2,1,0:T(8,128)} fusion(bf16[16,2,2,384,192]{4,3,2,1,0:T(8,128)(2,1)} %all-gather.3.cloned.1.call-done, bf16[384,1536]{1,0:T(8,128)(2,1)S(1)} %copy-done, bf16[2,192,1536]{2,1,0:T(8,128)(2,1)S(1)} %bitcast.69, s32[]{:T(128)S(6)} %select_n.11), kind=kOutput, calls=%fused_computation.10 | convolution fusion | flops 18124111872 | bytes 86409216 | tf_op jit(solution)/shard_map/zpax,ay->zpxy/dot_general | solution.py:42
  339.0 61.5 %fusion.1 = (bf16[16,1,384,1536]{3,2,1,0:T(8,128)(2,1)}, bf16[16,1,384,1536]{3,2,1,0:T(8,128)(2,1)}) fusion(f32[16,2,384,1536]{3,2,1,0:T(8,128)} %convert_element_type.34, f32[16,2,384,1536]{3,2,1,0:T(8,128)} %fusion.6), kind=kLoop, calls=%fused_computation.3 | loop fusion | flops 132120576 | bytes 188743680 | tf_op jit(solution)/shard_map/convert
  400.5 26.7 %convert_bitcast_fusion.1 = bf16[16,2,384,384]{2,3,1,0:T(8,128)(2,1)} fusion(bf16[16,1,384,1536]{3,2,1,0:T(8,128)(2,1)} %get-tuple-element.6, bf16[16,1,384,1536]{3,2,1,0:T(8,128)(2,1)} %get-tuple-element.5, bf16[384,1536]{1,0:T(8,128)(2,1)S(1)} %copy-done), kind=kOutput, calls=%fused_computation.15 | convolution fusion | flops 14519107584 | bytes 48365568 | tf_op jit(solution)/shard_map/zpxy,ny->zpnx/dot_general | solution.py:56
  427.2 23.9 %copy.29 = bf16[16,2,384,384]{3,1,0,2:T(2,128)(2,1)} copy(bf16[16,2,384,384]{2,3,1,0:T(8,128)(2,1)} %convert_bitcast_fusion.1) | data formatting | bytes 18874368 | tf_op jit(solution)/shard_map/convert_element_type | solution.py:58
  451.1 214.1 %all_to_all.52 = bf16[16,2,384,384]{3,1,0,2:T(2,128)(2,1)} all-to-all(bf16[16,2,384,384]{3,1,0,2:T(2,128)(2,1)} %copy.29), channel_id=1, replica_groups=mesh['rep'=4,'mx'=2,'my'=4] {'my'}, dimensions={2} | all-to-all | bytes 18874368 | tf_op jit(solution)/shard_map/all_to_all | solution.py:59
  665.3 10.9 %copy.30 = bf16[16,2,384,384]{3,2,1,0:T(8,128)(2,1)} copy(bf16[16,2,384,384]{3,1,0,2:T(2,128)(2,1)} %all_to_all.52) | data formatting | bytes 18874368 | tf_op jit(solution)/shard_map/all_to_all | solution.py:59
  676.2 10.6 %copy.31 = bf16[16,2,96,4,384]{4,3,2,1,0:T(4,128)(2,1)} copy(bf16[16,2,96,4,384]{4,2,3,1,0:T(8,128)(2,1)} %bitcast.73) | data formatting | bytes 18874368 | tf_op jit(solution)/shard_map/all_to_all | solution.py:59
  686.8 15.9 %reshape.25 = bf16[16,2,96,1536,1]{3,2,1,0,4:T(8,128)(2,1)} reshape(bf16[16,2,96,4,384]{4,3,2,1,0:T(4,128)(2,1)} %copy.31) | data formatting | bytes 18874368 | tf_op jit(solution)/shard_map/all_to_all | solution.py:59
  702.7 10.2 %convert_bitcast_fusion.2 = bf16[16,2,2,96,192]{4,3,2,1,0:T(8,128)(2,1)} fusion(bf16[2,192,1536,1,1]{2,1,0,4,3:T(8,128)(2,1)S(1)} %bitcast.68, bf16[16,2,96,1536,1]{3,2,1,0,4:T(8,128)(2,1)} %reshape.25), kind=kOutput, calls=%fused_computation.16 | convolution fusion | flops 3625058304 | bytes 12976128 | tf_op jit(solution)/shard_map/zpax,slx->zpsal/dot_general | solution.py:60
  712.8 35.2 %copy.46 = bf16[16,2,2,96,192]{0,1,4,3,2:T(2,128)(2,1)} copy(bf16[16,2,2,96,192]{4,3,2,1,0:T(8,128)(2,1)} %convert_bitcast_fusion.2) | data formatting | bytes 4718592 | tf_op jit(solution)/shard_map/reshape | solution.py:63
  748.1 27.3 %reshape.30 = bf16[2,2,294912]{2,1,0:T(2,128)(2,1)S(1)} reshape(bf16[36864,2,16]{2,1,0:T(2,128)(2,1)} %bitcast.70) | data formatting | bytes 4718592
  775.3 30.9 %all_to_all.53 = bf16[2,2,294912]{2,1,0:T(2,128)(2,1)} all-to-all(bf16[2,2,294912]{2,1,0:T(2,128)(2,1)S(1)} %reshape.30), channel_id=1, replica_groups=mesh['rep'=4,'mx'=2,'my'=4] {'mx'}, dimensions={0} | all-to-all | bytes 4718592 | tf_op jit(solution)/shard_map/all_to_all | solution.py:66
  806.2 22.4 %reshape.31 = bf16[36864,2,16]{2,1,0:T(2,128)(2,1)} reshape(bf16[2,2,294912]{2,1,0:T(2,128)(2,1)} %all_to_all.53) | data formatting | bytes 4718592
  828.6 35.6 %copy.34 = bf16[2,16,2,18432]{3,1,0,2:T(8,128)(2,1)} copy(bf16[2,16,2,18432]{1,2,3,0:T(2,128)(2,1)} %bitcast.71) | data formatting | bytes 4718592 | tf_op jit(solution)/shard_map/all_to_all | solution.py:66
  864.2 0.0 all-gather.5.cloned.1.call-update
  864.2 62.8 %all-gather.5.cloned.1.call-done = bf16[128,2,18432]{2,0,1:T(8,128)(2,1)} async-done(((bf16[32,2,18432]{2,0,1:T(8,128)(2,1)}), bf16[128,2,18432]{2,0,1:T(8,128)(2,1)}) %all-gather.5.cloned.1.call-update) | async-done | bytes 9437200 | tf_op jit(solution)/shard_map/all_gather | solution.py:70
  927.0 12.6 %copy.35 = bf16[128,2,18432]{0,2,1:T(8,128)(2,1)} copy(bf16[128,2,18432]{2,0,1:T(8,128)(2,1)} %all-gather.5.cloned.1.call-done) | data formatting | bytes 18874368 | tf_op jit(solution)/shard_map/all_gather | solution.py:70
  939.6 13.8 %convert_bitcast_fusion = bf16[2,192,96,96]{1,3,2,0:T(8,128)(2,1)} fusion(bf16[128,2,96,192]{0,3,2,1:T(8,128)(2,1)} %bitcast.72, bf16[384,1536]{1,0:T(8,128)(2,1)S(1)} %copy-done, s32[]{:T(128)S(6)} %select_n.9, s32[]{:T(128)S(6)} %add.30), kind=kOutput, calls=%fused_computation.14 | convolution fusion | flops 909508608 | bytes 16539656 | tf_op jit(solution)/shard_map/zpba,nz->pabn/dot_general | solution.py:72
  953.3 13.9 %copy.36 = bf16[2,192,96,96]{3,2,1,0:T(8,128)(2,1)} copy(bf16[2,192,96,96]{1,3,2,0:T(8,128)(2,1)} %convert_bitcast_fusion) | data formatting | bytes 14155776 | tf_op jit(solution)/shard_map/convert_element_type | solution.py:73
Async XLA Ops:
  6.5 1.3 copy-start
  6.5 296.3 %all-gather.3.cloned.1.call-start = ((), (), s32[]{:S(2)}) async-start(), calls=%async_computation.3 | async-start | bytes 15728640 | tf_op jit(solution)/shard_map/all_gather | solution.py:38
  84.0 843.0 %all-gather.5.cloned.1.call-start = ((), (), s32[]{:S(2)}) async-start(), calls=%async_computation.4 | async-start | bytes 11796480 | tf_op jit(solution)/shard_map/all_gather | solution.py:70
Sparse Core Ops, SparseCore 0:
  84.1 218.6 all-gather.2
  864.3 62.6 all-gather.4
where the time goes:
time: 986 us; the launch traced here: 974 us
  blocking collectives  277 us (28%)
  waiting for transfers between devices  244 us (25%)
  local copies, waits for them, and re-layouts  228 us (23%)
  matrix products  112 us (11%)
  other arithmetic  99.4 us (10%)
  between operations  13.6 us (1%)
    all_to_all x1, blocking collectives, body(): lax.all_to_all(proj_columns, 'my', split_axis=2, concat_axis=3, tiled=True)  214 us
    all_gather x1, waiting for transfers between devices, body(): lax.all_gather(grouped, 'my', axis=3, tiled=True)  181 us
    all_gather x1, waiting for transfers between devices, body(): portion = lax.all_gather(gathered_rows, 'rep', axis=0, tiled=True)  62.8 us
    another operation x1, other arithmetic  61.5 us
    unnamed x4, local copies, waits for them, and re-layouts  50.9 us
    convert_element_type x1, other arithmetic, body(): noise_wide = noise_field.astype(jnp.float32)  37.8 us
    all_to_all x3, local copies, waits for them, and re-layouts, body(): lax.all_to_all(proj_columns, 'my', split_axis=2, concat_axis=3, tiled=True)  37.4 us
    dot_general x1, matrix products, body(): jnp.einsum('zpax,ay->zpxy', block_part, mode_table, preferred_element_typ...  36.1 us
  transfers between devices with their start and end apart: 2, of which 2 were waited for; matrix products, arithmetic and copies ran while one was open for 4% of the time, Pallas kernels for 0%

commit v1 on v0

--- a/solution.py
+++ b/solution.py
@@ -67,7 +67,12 @@
     slab_back = lax.dynamic_slice_in_dim(mode_table, rep_index * own_block, own_block, 0)[
         :, slab_first : slab_first + planes_all
     ]
-    portion = lax.all_gather(gathered_rows, "rep", axis=0, tiled=True)
+    ring = [gathered_rows]
+    for hop in range(3):
+        ring.append(lax.ppermute(ring[-1], "rep", [(dev, (dev + 1) % 4) for dev in range(4)]))
+    portion = jnp.roll(
+        jnp.concatenate(ring[::-1], axis=0), (lax.axis_index("rep") + 1) * ring[0].shape[0], axis=0
+    )
     plane_grid = portion.reshape(portion.shape[0], 2, col_block, row_block)
     summed = jnp.einsum("zpba,nz->pabn", plane_grid, slab_back, preferred_element_type=jnp.float32)
     return summed.astype(jnp.bfloat16)

time: 986 us -> 1040 us (1.055)
  local copies, waits for them, and re-layouts: 228 us -> 258 us
  waiting for transfers between devices: 244 us -> 266 us
    ppermute x0 -> x3, waiting for transfers between devices: none -> 85.2 us  [body(): lax.ppermute(ring[-1], 'rep', [(dev, (dev + 1) % 4) for dev in range(4)])]
    all_gather x1 -> x0, waiting for transfers between devices: 62.8 us -> none  [body(): portion = lax.all_gather(gathered_rows, 'rep', axis=0, tiled=True)]
    dynamic_slice x0 -> x2, local copies, waits for them, and re-layouts: none -> 21.3 us  [body(): jnp.roll(jnp.concatenate(ring[::-1], axis=0), (lax.axis_index('rep') + 1)...]
    unnamed x4 -> x15, local copies, waits for them, and re-layouts: 50.9 us -> 71.4 us
    all_gather x1 -> x0, local copies, waits for them, and re-layouts: 12.6 us -> none  [body(): portion = lax.all_gather(gathered_rows, 'rep', axis=0, tiled=True)]
  transfers between devices with their start and end apart: 2 -> 4, of which waited for: 2 -> 4; matrix products, arithmetic and copies ran while one was open for 4% -> 4% of each run, Pallas kernels for 0% -> 0%
where the time goes in v1:
time: 1040 us; the launch traced here: 1030 us
  blocking collectives  277 us (27%)
  waiting for transfers between devices  266 us (26%)
  local copies, waits for them, and re-layouts  258 us (25%)
  matrix products  112 us (11%)
  other arithmetic  99.5 us (10%)
  between operations  13.7 us (1%)
    all_to_all x1, blocking collectives, body(): lax.all_to_all(proj_columns, 'my', split_axis=2, concat_axis=3, tiled=True)  214 us
    all_gather x1, waiting for transfers between devices, body(): lax.all_gather(grouped, 'my', axis=3, tiled=True)  181 us
    ppermute x3, waiting for transfers between devices, body(): lax.ppermute(ring[-1], 'rep', [(dev, (dev + 1) % 4) for dev in range(4)])  85.2 us
    unnamed x15, local copies, waits for them, and re-layouts  71.4 us
    another operation x1, other arithmetic  61.6 us
    convert_element_type x1, other arithmetic, body(): noise_wide = noise_field.astype(jnp.float32)  38 us
    all_to_all x3, local copies, waits for them, and re-layouts, body(): lax.all_to_all(proj_columns, 'my', split_axis=2, concat_axis=3, tiled=True)  37.3 us
    dot_general x1, matrix products, body(): jnp.einsum('zpax,ay->zpxy', block_part, mode_table, preferred_element_typ...  36.1 us
  transfers between devices with their start and end apart: 4, of which 4 were waited for; matrix products, arithmetic and copies ran while one was open for 4% of the time, Pallas kernels for 0%

profile of v1, /device:TPU:0, one launch (start us, length us, event | category | flops | bytes accessed | tf_op | source)
XLA Modules:
  0.0 1026.5 jit_solution(9667089754857323255)
XLA Ops:
  6.5 0.0 copy-start
  6.5 0.0 all-gather.2.cloned.1.call-start
  6.5 1.3 copy-done
  7.8 25.5 %convert_bitcast_fusion.3 = bf16[32,2,96,192]{2,0,3,1:T(8,128)(2,1)} fusion(bf16[2,192,96,384]{3,2,1,0:T(8,128)(2,1)} %param.3, bf16[384,1536]{1,0:T(8,128)(2,1)S(1)} %copy-done, s32[]{:T(128)S(6)} %select_n.23), kind=kOutput, calls=%fused_computation.17 | convolution fusion | flops 907149312 | bytes 30769156 | tf_op jit(solution)/shard_map/pabk,kz->zpba/dot_general | solution.py:28
  33.3 5.1 copy.45
  38.5 6.9 reshape.28
  45.3 31.9 %all_to_all.51 = bf16[32,2,18432]{2,1,0:T(2,128)(2,1)S(1)} all-to-all(bf16[32,2,18432]{2,1,0:T(2,128)(2,1)S(1)} %reshape.28), channel_id=1, replica_groups=mesh['rep'=4,'mx'=2,'my'=4] {'mx'}, dimensions={0} | all-to-all | bytes 4718592 | tf_op jit(solution)/shard_map/all_to_all | solution.py:32
  77.2 2.4 copy.52
  79.7 4.5 reshape.17
  84.1 0.0 all-gather.2.cloned.1.call-update
  84.2 38.0 %convert_element_type.34 = f32[16,2,384,1536]{3,2,1,0:T(8,128)} convert(bf16[16,2,384,1536]{3,2,1,0:T(8,128)(2,1)} %param.4) | non-fusion elementwise | flops 18874368 | bytes 113246208 | tf_op jit(solution)/shard_map/convert_element_type | solution.py:48
  122.1 180.9 %all-gather.2.cloned.1.call-done = bf16[16,2,2,384,192]{4,3,2,1,0:T(8,128)(2,1)} async-done(((bf16[16,2,2,96,192]{4,3,2,1,0:T(8,128)(2,1)}), bf16[16,2,2,384,192]{4,3,2,1,0:T(8,128)(2,1)}) %all-gather.2.cloned.1.call-update) | async-done | bytes 9437200 | tf_op jit(solution)/shard_map/all_gather | solution.py:38
  303.0 36.1 %fusion.6 = f32[16,2,384,1536]{3,2,1,0:T(8,128)} fusion(bf16[16,2,2,384,192]{4,3,2,1,0:T(8,128)(2,1)} %all-gather.2.cloned.1.call-done, bf16[384,1536]{1,0:T(8,128)(2,1)S(1)} %copy-done, bf16[2,192,1536]{2,1,0:T(8,128)(2,1)S(1)} %bitcast.69, s32[]{:T(128)S(6)} %select_n.24), kind=kOutput, calls=%fused_computation.10 | convolution fusion | flops 18124111872 | bytes 86409216 | tf_op jit(solution)/shard_map/zpax,ay->zpxy/dot_general | solution.py:42
  339.1 61.6 %fusion.1 = (bf16[16,1,384,1536]{3,2,1,0:T(8,128)(2,1)}, bf16[16,1,384,1536]{3,2,1,0:T(8,128)(2,1)}) fusion(f32[16,2,384,1536]{3,2,1,0:T(8,128)} %convert_element_type.34, f32[16,2,384,1536]{3,2,1,0:T(8,128)} %fusion.6), kind=kLoop, calls=%fused_computation.3 | loop fusion | flops 132120576 | bytes 188743680 | tf_op jit(solution)/shard_map/convert
  400.7 26.5 %convert_bitcast_fusion.1 = bf16[16,2,384,384]{2,3,1,0:T(8,128)(2,1)} fusion(bf16[16,1,384,1536]{3,2,1,0:T(8,128)(2,1)} %get-tuple-element.6, bf16[16,1,384,1536]{3,2,1,0:T(8,128)(2,1)} %get-tuple-element.5, bf16[384,1536]{1,0:T(8,128)(2,1)S(1)} %copy-done), kind=kOutput, calls=%fused_computation.15 | convolution fusion | flops 14519107584 | bytes 48365568 | tf_op jit(solution)/shard_map/zpxy,ny->zpnx/dot_general | solution.py:56
  427.2 23.9 %copy.29 = bf16[16,2,384,384]{3,1,0,2:T(2,128)(2,1)} copy(bf16[16,2,384,384]{2,3,1,0:T(8,128)(2,1)} %convert_bitcast_fusion.1) | data formatting | bytes 18874368 | tf_op jit(solution)/shard_map/convert_element_type | solution.py:58
  451.1 214.3 %all_to_all.52 = bf16[16,2,384,384]{3,1,0,2:T(2,128)(2,1)} all-to-all(bf16[16,2,384,384]{3,1,0,2:T(2,128)(2,1)} %copy.29), channel_id=1, replica_groups=mesh['rep'=4,'mx'=2,'my'=4] {'my'}, dimensions={2} | all-to-all | bytes 18874368 | tf_op jit(solution)/shard_map/all_to_all | solution.py:59
  665.4 10.9 %copy.30 = bf16[16,2,384,384]{3,2,1,0:T(8,128)(2,1)} copy(bf16[16,2,384,384]{3,1,0,2:T(2,128)(2,1)} %all_to_all.52) | data formatting | bytes 18874368 | tf_op jit(solution)/shard_map/all_to_all | solution.py:59
  676.3 10.5 %copy.31 = bf16[16,2,96,4,384]{4,3,2,1,0:T(4,128)(2,1)} copy(bf16[16,2,96,4,384]{4,2,3,1,0:T(8,128)(2,1)} %bitcast.73) | data formatting | bytes 18874368 | tf_op jit(solution)/shard_map/all_to_all | solution.py:59
  686.8 15.9 %reshape.25 = bf16[16,2,96,1536,1]{3,2,1,0,4:T(8,128)(2,1)} reshape(bf16[16,2,96,4,384]{4,3,2,1,0:T(4,128)(2,1)} %copy.31) | data formatting | bytes 18874368 | tf_op jit(solution)/shard_map/all_to_all | solution.py:59
  702.7 10.1 convert_bitcast_fusion.2
  712.8 35.3 %copy.46 = bf16[16,2,2,96,192]{0,1,4,3,2:T(2,128)(2,1)} copy(bf16[16,2,2,96,192]{4,3,2,1,0:T(8,128)(2,1)} %convert_bitcast_fusion.2) | data formatting | bytes 4718592 | tf_op jit(solution)/shard_map/reshape | solution.py:63
  748.1 27.0 %reshape.30 = bf16[2,2,294912]{2,1,0:T(2,128)(2,1)S(1)} reshape(bf16[36864,2,16]{2,1,0:T(2,128)(2,1)} %bitcast.70) | data formatting | bytes 4718592
  775.1 30.9 %all_to_all.53 = bf16[2,2,294912]{2,1,0:T(2,128)(2,1)} all-to-all(bf16[2,2,294912]{2,1,0:T(2,128)(2,1)S(1)} %reshape.30), channel_id=1, replica_groups=mesh['rep'=4,'mx'=2,'my'=4] {'mx'}, dimensions={0} | all-to-all | bytes 4718592 | tf_op jit(solution)/shard_map/all_to_all | solution.py:66
  806.0 22.4 %reshape.31 = bf16[36864,2,16]{2,1,0:T(2,128)(2,1)} reshape(bf16[2,2,294912]{2,1,0:T(2,128)(2,1)} %all_to_all.53) | data formatting | bytes 4718592
  828.4 34.3 %copy.34 = bf16[2,16,2,18432]{3,1,0,2:T(8,128)(2,1)S(1)} copy(bf16[2,16,2,18432]{1,2,3,0:T(2,128)(2,1)} %bitcast.71) | data formatting | bytes 4718592 | tf_op jit(solution)/shard_map/all_to_all | solution.py:66
  862.7 0.1 collective-permute-start
  862.8 28.3 %collective-permute-done = bf16[32,2,18432]{2,0,1:T(8,128)(2,1)S(1)} collective-permute-done((bf16[32,2,18432]{2,0,1:T(8,128)(2,1)S(1)}, bf16[32,2,18432]{2,0,1:T(8,128)(2,1)S(1)}, u32[]{:S(2)}, u32[]{:S(2)}) %collective-permute-start) | collective-permute-done | bytes 2359328 | tf_op jit(solution)/shard_map/ppermute | solution.py:72
  891.0 0.0 copy-start.1
  891.0 1.4 copy-done.1
  892.4 0.0 collective-permute-start.1
  892.4 28.4 %collective-permute-done.1 = bf16[32,2,18432]{2,0,1:T(8,128)(2,1)} collective-permute-done((bf16[32,2,18432]{2,0,1:T(8,128)(2,1)S(1)}, bf16[32,2,18432]{2,0,1:T(8,128)(2,1)}, u32[]{:S(2)}, u32[]{:S(2)}) %collective-permute-start.1) | collective-permute-done | bytes 2359328 | tf_op jit(solution)/shard_map/ppermute | solution.py:72
  920.8 0.0 collective-permute-start.2
  920.8 0.0 copy-start.2
  920.8 28.6 %collective-permute-done.2 = bf16[32,2,18432]{2,0,1:T(8,128)(2,1)} collective-permute-done((bf16[32,2,18432]{2,0,1:T(8,128)(2,1)}, bf16[32,2,18432]{2,0,1:T(8,128)(2,1)}, u32[]{:S(2)}, u32[]{:S(2)}) %collective-permute-start.2) | collective-permute-done | bytes 2359328 | tf_op jit(solution)/shard_map/ppermute | solution.py:72
  949.4 3.3 constant_dynamic-update-slice_fusion.7
  952.6 3.3 constant_dynamic-update-slice_fusion.6
  955.9 3.2 constant_dynamic-update-slice_fusion.5
  959.1 1.5 constant_dynamic-update-slice_fusion.4
  960.7 3.2 constant_dynamic-update-slice_fusion.3
  963.9 3.2 constant_dynamic-update-slice_fusion.2
  967.1 0.0 copy-done.2
  967.1 1.6 constant_dynamic-update-slice_fusion.1
  968.8 1.6 constant_dynamic-update-slice_fusion
  970.4 8.4 constant_dynamic-slice_fusion
  978.8 12.9 %copy.35 = bf16[128,2,18432]{0,2,1:T(8,128)(2,1)} copy(bf16[128,2,18432]{2,0,1:T(8,128)(2,1)} %constant_dynamic-slice_fusion) | data formatting | bytes 18874368 | tf_op jit(solution)/shard_map/jit(_roll_dynamic)/dynamic_slice | solution.py:73
  991.7 13.8 %convert_bitcast_fusion = bf16[2,192,96,96]{1,3,2,0:T(8,128)(2,1)} fusion(bf16[128,2,96,192]{0,3,2,1:T(8,128)(2,1)} %bitcast.72, bf16[384,1536]{1,0:T(8,128)(2,1)S(1)} %copy-done, s32[]{:T(128)S(6)} %select_n.22, s32[]{:T(128)S(6)} %add.46), kind=kOutput, calls=%fused_computation.14 | convolution fusion | flops 909508608 | bytes 16539656 | tf_op jit(solution)/shard_map/zpba,nz->pabn/dot_general | solution.py:77
  1005.5 13.9 %copy.36 = bf16[2,192,96,96]{3,2,1,0:T(8,128)(2,1)} copy(bf16[2,192,96,96]{1,3,2,0:T(8,128)(2,1)} %convert_bitcast_fusion) | data formatting | bytes 14155776 | tf_op jit(solution)/shard_map/convert_element_type | solution.py:78
Async XLA Ops:
  6.5 1.3 copy-start
  6.5 296.5 %all-gather.2.cloned.1.call-start = ((), (), s32[]{:S(2)}) async-start(), calls=%async_computation.3 | async-start | bytes 15728640 | tf_op jit(solution)/shard_map/all_gather | solution.py:38
  862.7 28.3 %collective-permute-start = (bf16[32,2,18432]{2,0,1:T(8,128)(2,1)S(1)}, bf16[32,2,18432]{2,0,1:T(8,128)(2,1)S(1)}, u32[]{:S(2)}, u32[]{:S(2)}) collective-permute-start(bf16[32,2,18432]{2,0,1:T(8,128)(2,1)S(1)} %bitcast.74), channel_id=1, source_target_pairs={{0,8},{8,16},{16,24},{24,0},{1,9},{9,17},{17,25},{25,1},{2,10},{10... | collective-permute-start | bytes 7077896 | tf_op jit(solution)/shard_map/ppermute | solution.py:72
  891.0 1.4 copy-start.1
  892.4 28.4 %collective-permute-start.1 = (bf16[32,2,18432]{2,0,1:T(8,128)(2,1)S(1)}, bf16[32,2,18432]{2,0,1:T(8,128)(2,1)}, u32[]{:S(2)}, u32[]{:S(2)}) collective-permute-start(bf16[32,2,18432]{2,0,1:T(8,128)(2,1)S(1)} %collective-permute-done), channel_id=1, source_target_pairs={{0,8},{8,16},{16,24},{24,0},{1,9},{9,17},{17,25},{25,1},{2,10},{10... | collective-permute-start | bytes 7077896 | tf_op jit(solution)/shard_map/ppermute | solution.py:72
  920.8 28.6 %collective-permute-start.2 = (bf16[32,2,18432]{2,0,1:T(8,128)(2,1)}, bf16[32,2,18432]{2,0,1:T(8,128)(2,1)}, u32[]{:S(2)}, u32[]{:S(2)}) collective-permute-start(bf16[32,2,18432]{2,0,1:T(8,128)(2,1)} %collective-permute-done.1), channel_id=1, source_target_pairs={{0,8},{8,16},{16,24},{24,0},{1,9},{9,17},{17,25},{25,1},{2,10},{10... | collective-permute-start | bytes 7077896 | tf_op jit(solution)/shard_map/ppermute | solution.py:72
  920.8 46.3 %copy-start.2 = (bf16[32,2,18432]{2,0,1:T(8,128)(2,1)S(1)}, bf16[32,2,18432]{2,0,1:T(8,128)(2,1)}, u32[]{:S(2)}) copy-start(bf16[32,2,18432]{2,0,1:T(8,128)(2,1)} %copy-done.1) | copy-start | bytes 7077892
Sparse Core Ops, SparseCore 0:
  84.3 218.6 all-gather.1
